TPU v7x, 32 devices: a whole 2x2x4 slice. The times are simulated.
32 devices in a mesh: rep: 4 (over x, y), dp: 8 (over z, core).
Axes of the slice: x: 2, y: 2, z: 4, core: 2. Of those that a mesh axis runs over, the one named last changes fastest.
Arguments:
- a: bfloat16 [32, 4, 8192, 1024], P(('rep', 'dp')), parts along dimension 0
- g: bfloat16 [32, 4, 8192, 2816], P(('rep', 'dp')), parts along dimension 0
Outputs:
- output: bfloat16 [16, 1024, 2816], P('rep'), parts along dimension 0
There are 4 independent parts. A program takes and returns all parts, laid end to end along the dimension named above; each array names one.
All inputs are finite; a program needn't handle non-finite values.
Results may differ from a plain program's by a relative error of at most 0.012.
Values are sent between devices in bfloat16 or wider.
A program may use at most 2 GiB of HBM per device.

v0:
```python
import jax
import jax.numpy as jnp


def solution(mesh):
    groups = mesh.shape["rep"]

    def step(a, g):
        a, g = (t.reshape(groups, -1, *t.shape[1:]) for t in (a, g))
        sums = jnp.einsum("rsntd,rsntf->rndf", a, g, preferred_element_type=jnp.float32)
        return sums.astype(jnp.bfloat16).reshape(-1, *sums.shape[2:])

    return step
```

profile of v0, /device:TPU:0, one launch (start us, length us, event | category | flops | bytes accessed | tf_op | source)
XLA Modules:
  0.0 1100.7 jit_solution(12239937989242120052)
XLA Ops:
  0.0 211.9 %fusion.3 = f32[1,4,1024,2816]{3,2,1,0:T(8,128)} fusion(bf16[1,4,8192,2816]{3,2,1,0:T(8,128)(2,1)} %param.1, bf16[1,4,8192,1024]{3,2,1,0:T(8,128)(2,1)} %param), kind=kOutput, calls=%fused_computation.3 | convolution fusion | flops 188978561024 | bytes 297795584 | tf_op jit(solution)/rsntd,rsntf->rndf/dot_general | solution.py:10
  211.9 888.9 %all-reduce.2 = bf16[1,4,1024,2816]{3,2,1,0:T(8,128)(2,1)} all-reduce(f32[1,4,1024,2816]{3,2,1,0:T(8,128)} %fusion.3), channel_id=1, replica_groups=[4,8]<=[32], use_global_device_ids=true, to_apply=%add.clone | all-reduce | flops 11534336 | bytes 69206016 | tf_op jit(solution)/rsntd,rsntf->rndf/dot_general | solution.py:10
where the time goes:
time: 1100 us
  blocking collectives  889 us (81%)
  matrix products  212 us (19%)
    dot_general x1, blocking collectives, step(): jnp.einsum('rsntd,rsntf->rndf', a, g, preferred_element_type=jnp.float32)  889 us
    dot_general x1, matrix products, step(): jnp.einsum('rsntd,rsntf->rndf', a, g, preferred_element_type=jnp.float32)  212 us

commit v1 on v0

v1 whole, which is shorter than its diff:
```python
import functools

import jax
import jax.numpy as jnp
from jax import lax
from jax.experimental import pallas as pl
from jax.experimental.pallas import tpu as pltpu
from jax.sharding import PartitionSpec as P

MESH = pl.DeviceIdType.MESH
BF16, F32 = jnp.bfloat16, jnp.float32

T, D, F, NM = 8192, 1024, 2816, 4
TM, TN, H = 512, 256, 256
KB = 512
NA = 4
KS = T // 256
R, J = D // TM, F // TN
SM = R * J
S = NM * SM
NB = T // KB
NR = 16
NP = 8
NS = 4
LX, LE, LM, LF, LG, LH = 2, 4, 6, 8, 10, 12


def kernel(a, g, o, at0, at1, gbuf, araw, pb, xs, xr, es, er, mr, fs, asem, gsem,
           xss, xrs, ess, ers, mrs, fss, frs, gss, hrs):
    me = lax.axis_index("dp")
    z, c = me // 2, lax.rem(me, 2)
    end = (z == 0) | (z == 3)
    mid = (z == 1) | (z == 2)
    ats = (at0, at1)

    def dev(zz, cc):
        return {"dp": zz * 2 + cc}

    z_mid = jnp.where(z == 0, 1, 2)
    z_end = jnp.where(z == 1, 0, 3)
    z_other = jnp.where(z == 1, 2, 1)
    inward = jnp.where(end, z_mid, z_other)
    sibling = dev(z, 1 - c)

    def acopy(n, b):
        return pltpu.make_async_copy(a.at[n, pl.ds(b * KB, KB), :], araw.at[lax.rem(b, NA)], asem.at[lax.rem(b, NA)])

    def gcopy(u):
        cols = pl.ds(pl.multiple_of(lax.rem(u, J) * TN, TN), TN)
        return pltpu.make_async_copy(g.at[u // J, :, cols], gbuf.at[lax.rem(u, 2)], gsem.at[lax.rem(u, 2)])

    def turn(dst, b, i):
        ti, di = i % (KB // 256), i // (KB // 256)
        dst[b * (KB // 256) + ti, pl.ds(di * 256, 256), :] = araw[
            lax.rem(b, NA), pl.ds(ti * 256, 256), pl.ds(di * 256, 256)].T

    def place(u, h):
        q = lax.rem(u, SM)
        rows = pl.ds(pl.multiple_of(lax.rem(q, R) * TM + h * H, H), H)
        return o.at[u // SM, rows, pl.ds(pl.multiple_of(q // R * TN, TN), TN)]

    def remote(src, dst, send, recv, device):
        return pltpu.make_async_remote_copy(
            src_ref=src, dst_ref=dst, send_sem=send, recv_sem=recv, device_id=device, device_id_type=MESH)

    def xcopy(u):
        i, k = lax.rem(u, NR), lax.rem(u, NS)
        return remote(xs.at[k], xr.at[i], xss.at[k], xrs.at[i], sibling)

    def ecopy(u):
        i, k = lax.rem(u, NR), lax.rem(u, NS)
        return remote(es.at[k], er.at[i], ess.at[k], ers.at[i], dev(inward, c))

    def mcopy(u):
        i, k = lax.rem(u, NR), lax.rem(u, NS)
        return remote(es.at[k], mr.at[i], ess.at[k], mrs.at[i], dev(inward, c))

    def fcopies(u):
        i, k = lax.rem(u, NR), lax.rem(u, NS)
        return (
            remote(fs.at[k], place(u, c), fss.at[k, 0], frs.at[i], dev(z_end, c)),
            remote(fs.at[k], place(u, c), fss.at[k, 1], frs.at[i], dev(z_other, c)),
            remote(fs.at[k], place(u, c), fss.at[k, 2], hrs.at[i], sibling),
        )

    def fkeep(u):
        k = lax.rem(u, NS)
        return pltpu.make_async_copy(fs.at[k], place(u, c), fss.at[k, 3])

    def onward(u):
        i, k = lax.rem(u, NR), lax.rem(u, NS)
        return remote(place(u, c), place(u, c), gss.at[k, 0], frs.at[i], dev(z_end, c))

    def across(u):
        i, k = lax.rem(u, NR), lax.rem(u, NS)
        return remote(place(u, c), place(u, c), gss.at[k, 1], hrs.at[i], sibling)

    def mine(u):
        return z == 1 + lax.rem(u, 2)

    def chip_sum(u):
        return pb[lax.rem(u, NP), pl.ds(pl.multiple_of(c * H, H), H), :] + xr[lax.rem(u, NR)].astype(F32)

    def live(u, top=S):
        return (u >= 0) & (u < top)

    def stage_x(u):
        @pl.when(live(u - NS))
        def _():
            xcopy(u - NS).wait_send()

        @pl.when(live(u))
        def _():
            xs[lax.rem(u, NS)] = pb[lax.rem(u, NP), pl.ds(pl.multiple_of((1 - c) * H, H), H), :].astype(BF16)
            xcopy(u).start()

    def stage_end(u):
        @pl.when(end & live(u - NS))
        def _():
            ecopy(u - NS).wait_send()

        @pl.when(end & live(u))
        def _():
            xcopy(u).wait_recv()
            es[lax.rem(u, NS)] = chip_sum(u).astype(BF16)
            ecopy(u).start()

    def stage_pass(u):
        pass_on = mid & ~mine(u)

        @pl.when(pass_on & live(u - NS))
        def _():
            mcopy(u - NS).wait_send()

        @pl.when(pass_on & live(u))
        def _():
            xcopy(u).wait_recv()
            ecopy(u).wait_recv()
            es[lax.rem(u, NS)] = (chip_sum(u) + er[lax.rem(u, NR)].astype(F32)).astype(BF16)
            mcopy(u).start()

    def stage_own(u):
        @pl.when(mid & mine(u) & live(u - NS))
        def _():
            for copy in fcopies(u - NS):
                copy.wait_send()
            fkeep(u - NS).wait()

        @pl.when(mid & mine(u) & live(u))
        def _():
            xcopy(u).wait_recv()
            ecopy(u).wait_recv()
            mcopy(u).wait_recv()
            i = lax.rem(u, NR)
            fs[lax.rem(u, NS)] = (chip_sum(u) + er[i].astype(F32) + mr[i].astype(F32)).astype(BF16)
            for copy in fcopies(u):
                copy.start()
            fkeep(u).start()

    def stage_forward(u):
        pass_on = mid & ~mine(u)

        @pl.when(pass_on & live(u - NS))
        def _():
            onward(u - NS).wait_send()
            across(u - NS).wait_send()

        @pl.when(pass_on & live(u))
        def _():
            onward(u).wait_recv()
            onward(u).start()
            across(u).start()

    def stage_last(u):
        @pl.when(end & live(u - NS))
        def _():
            across(u - NS).wait_send()

        @pl.when(end & live(u))
        def _():
            onward(u).wait_recv()
            across(u).start()

    def stage_home(u):
        @pl.when(live(u))
        def _():
            across(u).wait_recv()

    def serve(s):
        stage_end(s - LX)
        stage_own(s - LM)
        stage_forward(s - LF)
        stage_pass(s - LE)
        stage_last(s - LG)
        stage_home(s - LH)

    barrier = pltpu.get_barrier_semaphore()
    pl.semaphore_signal(barrier, inc=1, device_id=sibling, device_id_type=MESH)

    @pl.when(z > 0)
    def _():
        pl.semaphore_signal(barrier, inc=1, device_id=dev(z - 1, c), device_id_type=MESH)

    @pl.when(z < 3)
    def _():
        pl.semaphore_signal(barrier, inc=1, device_id=dev(z + 1, c), device_id_type=MESH)

    for b in range(NA):
        acopy(0, b).start()
    gcopy(0).start()

    def first(b, _):
        acopy(0, b).wait()
        for i in range(8):
            turn(at0, b, i)

        @pl.when(b + NA < NB)
        def _():
            acopy(0, b + NA).start()
        return 0

    lax.fori_loop(0, NB, first, 0)
    for b in range(NA - 1):
        acopy(1, b).start()

    @pl.when(end)
    def _():
        pl.semaphore_wait(barrier, 2)

    @pl.when(mid)
    def _():
        pl.semaphore_wait(barrier, 3)

    for n in range(NM):
        now, later = ats[n % 2], ats[(n + 1) % 2]

        def step(q, _, n=n, now=now, later=later):
            s = n * SM + q
            j, r = q // R, lax.rem(q, R)
            u = n * J + j

            @pl.when(r == 0)
            def _():
                gcopy(u).wait()

                @pl.when(u + 1 < NM * J)
                def _():
                    gcopy(u + 1).start()

            b = jnp.minimum(q, NB - 1)
            if n < NM - 1:
                @pl.when(q < NB)
                def _():
                    acopy(n + 1, b).wait()

                @pl.when(q + NA - 1 < NB)
                def _():
                    acopy(n + 1, b + NA - 1).start()

            if n < NM - 2:
                @pl.when(q + NA - 1 >= SM)
                def _():
                    acopy(n + 2, q + NA - 1 - SM).start()

            serve(s)
            if n < NM - 1:
                for i in range(8):
                    turn(later, b, i)
            rows = pl.ds(pl.multiple_of(r * TM, TM), TM)
            lhs = jnp.concatenate([now[k, rows, :] for k in range(KS)], axis=1)
            pb[lax.rem(s, NP)] = jnp.dot(lhs, gbuf[lax.rem(u, 2)], preferred_element_type=F32)
            stage_x(s)
            return 0

        lax.fori_loop(0, SM, step, 0)

    def drain(s, _):
        stage_x(s)
        serve(s)
        return 0

    lax.fori_loop(S, S + LH + NS, drain, 0)


def solution(mesh):
    dma = pltpu.SemaphoreType.DMA

    def sums(a, g):
        return pl.pallas_call(
            kernel,
            out_shape=jax.ShapeDtypeStruct((NM, D, F), BF16),
            in_specs=[pl.BlockSpec(memory_space=pltpu.HBM)] * 2,
            out_specs=pl.BlockSpec(memory_space=pltpu.HBM),
            scratch_shapes=[
                pltpu.VMEM((KS, D, 256), BF16),
                pltpu.VMEM((KS, D, 256), BF16),
                pltpu.VMEM((2, T, TN), BF16),
                pltpu.VMEM((NA, KB, D), BF16),
                pltpu.VMEM((NP, TM, TN), F32),
                pltpu.VMEM((NS, H, TN), BF16),
                pltpu.VMEM((NR, H, TN), BF16),
                pltpu.VMEM((NS, H, TN), BF16),
                pltpu.VMEM((NR, H, TN), BF16),
                pltpu.VMEM((NR, H, TN), BF16),
                pltpu.VMEM((NS, H, TN), BF16),
                dma((NA,)), dma((2,)),
                dma((NS,)), dma((NR,)),
                dma((NS,)), dma((NR,)), dma((NR,)),
                dma((NS, 4)), dma((NR,)), dma((NS, 2)), dma((NR,)),
            ],
            compiler_params=pltpu.CompilerParams(
                collective_id=1, has_side_effects=True, vmem_limit_bytes=67043328),
            name="sums",
        )(a, g)

    def step(a, g):
        return jax.shard_map(
            lambda a, g: sums(a[0], g[0]), mesh=mesh,
            in_specs=(P(("rep", "dp")), P(("rep", "dp"))), out_specs=P("rep"), check_vma=False)(a, g)

    return step
```

time: 1100 us -> 302 us (0.27)
  blocking collectives: 889 us -> 0 us
  Pallas kernels: 0 us -> 282 us
  matrix products: 212 us -> 0 us
  local copies, waits for them, and re-layouts: 0 us -> 19.8 us
    dot_general x1 -> x0, blocking collectives: 889 us -> none  [step(): jnp.einsum('rsntd,rsntf->rndf', a, g, preferred_element_type=jnp.float32)]
    pallas_call x0 -> x1, Pallas kernels: none -> 282 us  [sums(): pl.pallas_call(kernel, out_shape=jax.ShapeDtypeStruct((NM, D, F), BF16),...]
    dot_general x1 -> x0, matrix products: 212 us -> none  [step(): jnp.einsum('rsntd,rsntf->rndf', a, g, preferred_element_type=jnp.float32)]
    unnamed x0 -> x1, local copies, waits for them, and re-layouts: none -> 19.8 us
where the time goes in v1:
time: 302 us
  Pallas kernels  282 us (93%)
  local copies, waits for them, and re-layouts  19.8 us (7%)
    pallas_call x1, Pallas kernels, sums(): pl.pallas_call(kernel, out_shape=jax.ShapeDtypeStruct((NM, D, F), BF16),...  282 us
    unnamed x1, local copies, waits for them, and re-layouts  19.8 us

profile of v1, /device:TPU:0, one launch (start us, length us, event | category | flops | bytes accessed | tf_op | source)
XLA Modules:
  0.0 301.7 jit_solution(6200279322422385997)
XLA Ops:
  0.0 281.9 %sums.1 = bf16[4,1024,2816]{2,1,0:T(8,128)(2,1)} custom-call(bf16[4,8192,1024]{2,1,0:T(8,128)(2,1)} %bitcast.a, bf16[4,8192,2816]{2,1,0:T(8,128)(2,1)} %bitcast.1.g), custom_call_target="tpu_custom_call" | custom-call | tf_op jit(solution)/shard_map/sums/pallas_call | solution.py:289
  281.9 19.8 %copy.4 = bf16[4,1024,2816]{2,1,0:T(8,128)(2,1)} copy(bf16[4,1024,2816]{2,1,0:T(8,128)(2,1)} %sums.1) | data formatting | bytes 46137344

commit v2 on v1

v2 whole, which is shorter than its diff:
```python
import jax
import jax.numpy as jnp
from jax import lax
from jax.experimental import pallas as pl
from jax.experimental.pallas import tpu as pltpu
from jax.sharding import PartitionSpec as P

MESH = pl.DeviceIdType.MESH
BF16, F32 = jnp.bfloat16, jnp.float32

T, D, F, NM = 8192, 1024, 2816, 4
TM, TN = 512, 256
H = TM // 2
KT = 256
KS = T // KT
HB = TM // KT
KB = 512
NB = T // KB
KD = 8
NA = 2
NO = 4
R, J = D // TM, F // TN
SM = R * J
RUN = NM
S = RUN * SM
SX = (NM - 1) * SM
NX, NE, NM2 = 11, 10, 4
NF = 16
NP = 7
NS = 4
LX, LE, LM, LF, LG, LH = 2, 4, 6, 8, 10, 12


def kernel(a, g, x, o, at1, gbuf, araw, pb, xs, xr, es, er, mr, fs, hsem, asem, gsem,
           xss, xrs, ess, ers, mrs, fss, frs, gss, hrs, osem):
    me = lax.axis_index("dp")
    z, c = me // 2, lax.rem(me, 2)
    end = (z == 0) | (z == 3)
    mid = (z == 1) | (z == 2)

    def dev(zz, cc):
        return {"dp": zz * 2 + cc}

    z_mid = jnp.where(z == 0, 1, 2)
    z_end = jnp.where(z == 1, 0, 3)
    z_other = jnp.where(z == 1, 2, 1)
    inward = dev(jnp.where(end, z_mid, z_other), c)
    sibling = dev(z, 1 - c)

    def even(k, rows):
        return x.at[k // J, rows, pl.ds(pl.multiple_of(k % J * TN, TN), TN)]

    def odd(k, rows):
        return at1.at[k, rows, :]

    ats = (even, odd)

    def acopy(n, b):
        i = lax.rem(b, NA)
        return pltpu.make_async_copy(a.at[n, pl.ds(b * KB, KB), :], araw.at[i], asem.at[i])

    def gcopy(u):
        cols = pl.ds(pl.multiple_of(lax.rem(u, J) * TN, TN), TN)
        return pltpu.make_async_copy(g.at[u // J, :, cols], gbuf.at[lax.rem(u, 2)], gsem.at[lax.rem(u, 2)])

    def hcopy(i, k):
        rows = pl.ds(i * KT, KT)
        return pltpu.make_async_copy(a.at[0, pl.ds(k * KT, KT), rows], at1.at[k, rows, :], hsem.at[i, k])

    def dot(at, rows, gb):
        total = None
        for k in range(0, KS, KD):
            lhs = jnp.concatenate([at(i, rows)[...] for i in range(k, k + KD)], axis=1)
            term = jnp.dot(lhs, gb[pl.ds(k * KT, KD * KT), :], preferred_element_type=F32)
            total = term if total is None else total + term
        return total

    def remote(src, dst, send, recv, device):
        return pltpu.make_async_remote_copy(
            src_ref=src, dst_ref=dst, send_sem=send, recv_sem=recv, device_id=device, device_id_type=MESH)


    def xcopy(u):
        i, k = lax.rem(u, NX), lax.rem(u, 2)
        return remote(xs.at[k], xr.at[i], xss.at[k], xrs.at[i], sibling)

    def ecopy(u):
        i, k = lax.rem(u, NE), lax.rem(u, NS)
        return remote(es.at[k], er.at[i], ess.at[k], ers.at[i], inward)

    def mcopy(u):
        i, k = lax.rem(u // 2, NM2), lax.rem(u, NS)
        return remote(es.at[k], mr.at[i], ess.at[k], mrs.at[i], inward)

    def fcopies(u, at):
        i, k = lax.rem(u, NF), lax.rem(u, NS)
        return (
            remote(fs.at[k], at, fss.at[k, 0], frs.at[i], dev(z_end, c)),
            remote(fs.at[k], at, fss.at[k, 1], frs.at[i], dev(z_other, c)),
            remote(fs.at[k], at, fss.at[k, 2], hrs.at[i], sibling),
        )

    def fkeep(u, at):
        k = lax.rem(u, NS)
        return pltpu.make_async_copy(fs.at[k], at, fss.at[k, 3])

    def onward(u, at):
        i, k = lax.rem(u, NF), lax.rem(u, NS)
        return remote(at, at, gss.at[k, 0], frs.at[i], dev(z_end, c))

    def across(u, at):
        i, k = lax.rem(u, NF), lax.rem(u, NS)
        return remote(at, at, gss.at[k, 1], hrs.at[i], sibling)

    def placed(u, do):
        q = lax.rem(u, SM)
        rows = pl.ds(pl.multiple_of(lax.rem(q, R) * TM + c * H, H), H)
        cols = pl.ds(pl.multiple_of(q // R * TN, TN), TN)

        @pl.when(u < SX)
        def _():
            do(o.at[u // SM, rows, cols])

        @pl.when(u >= SX)
        def _():
            do(x.at[NM - 1, rows, cols])

    def mine(u):
        return z == 1 + lax.rem(u, 2)

    def chip_sum(u):
        return pb[lax.rem(u, NP), pl.ds(pl.multiple_of(c * H, H), H), :] + xr[lax.rem(u, NX)].astype(F32)

    def live(u):
        return (u >= 0) & (u < S)

    def stage_x(u):
        @pl.when(live(u - 2))
        def _():
            xcopy(u - 2).wait_send()

        @pl.when(live(u))
        def _():
            xs[lax.rem(u, 2)] = pb[lax.rem(u, NP), pl.ds(pl.multiple_of((1 - c) * H, H), H), :].astype(BF16)
            xcopy(u).start()

    def stage_end(u):
        @pl.when(end & live(u - NS))
        def _():
            ecopy(u - NS).wait_send()

        @pl.when(end & live(u))
        def _():
            xcopy(u).wait_recv()
            es[lax.rem(u, NS)] = chip_sum(u).astype(BF16)
            ecopy(u).start()

    def stage_pass(u):
        pass_on = mid & ~mine(u)

        @pl.when(pass_on & live(u - NS))
        def _():
            mcopy(u - NS).wait_send()

        @pl.when(pass_on & live(u))
        def _():
            xcopy(u).wait_recv()
            ecopy(u).wait_recv()
            es[lax.rem(u, NS)] = (chip_sum(u) + er[lax.rem(u, NE)].astype(F32)).astype(BF16)
            mcopy(u).start()

    def stage_own(u):
        k = lax.rem(u, NS)

        @pl.when(mid & mine(u) & live(u - NS))
        def _():
            for copy in fcopies(u - NS, er.at[0]):
                copy.wait_send()
            fkeep(u - NS, er.at[0]).wait()

        @pl.when(mid & mine(u) & live(u))
        def _():
            xcopy(u).wait_recv()
            ecopy(u).wait_recv()
            mcopy(u).wait_recv()
            fs[k] = (chip_sum(u) + er[lax.rem(u, NE)].astype(F32) + mr[lax.rem(u // 2, NM2)].astype(F32)).astype(BF16)

            def send(at):
                for copy in fcopies(u, at):
                    copy.start()
                fkeep(u, at).start()

            placed(u, send)

    def stage_forward(u):
        pass_on = mid & ~mine(u)

        @pl.when(pass_on & live(u - NS))
        def _():
            onward(u - NS, er.at[0]).wait_send()
            across(u - NS, er.at[0]).wait_send()

        @pl.when(pass_on & live(u))
        def _():
            onward(u, er.at[0]).wait_recv()

            def send(at):
                onward(u, at).start()
                across(u, at).start()

            placed(u, send)

    def stage_last(u):

        @pl.when(end & live(u - NS))
        def _():
            across(u - NS, er.at[0]).wait_send()

        @pl.when(end & live(u))
        def _():
            onward(u, er.at[0]).wait_recv()
            placed(u, lambda at: across(u, at).start())

    def stage_home(u):
        @pl.when(live(u))
        def _():
            across(u, er.at[0]).wait_recv()

    def serve(s):
        stage_end(s - LX)
        stage_own(s - LM)
        stage_forward(s - LF)
        stage_pass(s - LE)
        stage_last(s - LG)
        stage_home(s - LH)

    def take(p):
        cols = pl.ds(pl.multiple_of(lax.rem(p, J) * TN, TN), TN)
        at = (p // J, slice(None), cols)
        return pltpu.make_async_copy(o.at[at], x.at[at], osem.at[lax.rem(p, NO)])

    barrier = pltpu.get_barrier_semaphore()
    pl.semaphore_signal(barrier, inc=1, device_id=sibling, device_id_type=MESH)

    @pl.when(z > 0)
    def _():
        pl.semaphore_signal(barrier, inc=1, device_id=dev(z - 1, c), device_id_type=MESH)

    @pl.when(z < 3)
    def _():
        pl.semaphore_signal(barrier, inc=1, device_id=dev(z + 1, c), device_id_type=MESH)

    def fetch(r):
        def one(k, _):
            for i in range(r * HB, (r + 1) * HB):
                hcopy(i, k).start()
            return 0

        lax.fori_loop(0, KS, one, 0)

    def await_first(r, k):
        for i in range(r * HB, (r + 1) * HB):
            hcopy(i, k).wait()

    def turn_first(r, k):
        for i in range(r * HB, (r + 1) * HB):
            rows = pl.ds(i * KT, KT)
            even(k, rows)[...] = at1[k, rows, :].T

    fetch(0)
    gcopy(0).start()
    for r in range(1, R):
        fetch(r)
    for b in range(NA - 1 if RUN > 1 else 0):
        acopy(1, b).start()
    gcopy(1).start()

    def first(k, _):
        await_first(0, k)
        turn_first(0, k)
        return 0

    lax.fori_loop(0, KS, first, 0)

    @pl.when(end)
    def _():
        pl.semaphore_wait(barrier, 2)

    @pl.when(mid)
    def _():
        pl.semaphore_wait(barrier, 3)

    gcopy(0).wait()
    for r in range(R):
        serve(jnp.int32(r))
        if r < R - 1:
            for k in range(KS):
                await_first(r + 1, k)
            for k in range(KS):
                turn_first(r + 1, k)
        pb[r % NP] = dot(even, pl.ds(r * TM, TM), gbuf.at[0])
        stage_x(jnp.int32(r))

    for n in range(RUN):
        now, later = ats[n % 2], ats[(n + 1) % 2]

        def step(q, _, n=n, now=now, later=later):
            s = n * SM + q
            j, r = q // R, lax.rem(q, R)
            u = n * J + j

            @pl.when(r == 0)
            def _():
                gcopy(u).wait()

                @pl.when(u + 1 < RUN * J)
                def _():
                    gcopy(u + 1).start()

            q0 = R if n == 0 else 0
            b = jnp.minimum(q - q0, NB - 1)
            if n < RUN - 1:
                @pl.when(q - q0 < NB)
                def _():
                    acopy(n + 1, b).wait()

                @pl.when(q - q0 + NA - 1 < NB)
                def _():
                    acopy(n + 1, b + NA - 1).start()

            if n < RUN - 2:
                @pl.when(q + NA - 1 >= SM)
                def _():
                    acopy(n + 2, q + NA - 1 - SM).start()

            if n == NM - 1:
                for p in (2 * q, 2 * q + 1):
                    @pl.when((p >= NO) & (p - NO < SX // R))
                    def _(p=p):
                        take(p - NO).wait()

                    @pl.when(p < SX // R)
                    def _(p=p):
                        take(p).start()

            serve(s)
            if n < RUN - 1:
                for i in range(KB // KT):
                    for part in range(D // 256):
                        part = pl.ds(part * 256, 256)
                        later(b * (KB // KT) + i, part)[...] = araw[lax.rem(b, NA), pl.ds(i * KT, KT), part].T
            pb[lax.rem(s, NP)] = dot(now, pl.ds(pl.multiple_of(r * TM, TM), TM), gbuf.at[lax.rem(u, 2)])
            stage_x(s)
            return 0

        lax.fori_loop(R if n == 0 else 0, SM, step, 0)

    def drain(s, _):
        stage_x(s)
        serve(s)
        return 0

    lax.fori_loop(S, S + LH + NS, drain, 0)


def put(x, out, sem):
    copies = [pltpu.make_async_copy(x.at[n], out.at[n], sem.at[n]) for n in range(NM)]
    for copy in copies:
        copy.start()
    for copy in copies:
        copy.wait()


def solution(mesh):
    dma = pltpu.SemaphoreType.DMA

    def sums(a, g):
        x, _ = pl.pallas_call(
            kernel,
            out_shape=(pltpu.VMEM((NM, D, F), BF16), jax.ShapeDtypeStruct((NM - 1, D, F), BF16)),
            in_specs=[pl.BlockSpec(memory_space=pltpu.HBM)] * 2,
            out_specs=(pl.BlockSpec(memory_space=pltpu.VMEM), pl.BlockSpec(memory_space=pltpu.HBM)),
            scratch_shapes=[
                pltpu.VMEM((KS, D, KT), BF16),
                pltpu.VMEM((2, T, TN), BF16),
                pltpu.VMEM((NA, KB, D), BF16),
                pltpu.VMEM((NP, TM, TN), F32),
                pltpu.VMEM((2, H, TN), BF16),
                pltpu.VMEM((NX, H, TN), BF16),
                pltpu.VMEM((NS, H, TN), BF16),
                pltpu.VMEM((NE, H, TN), BF16),
                pltpu.VMEM((NM2, H, TN), BF16),
                pltpu.VMEM((NS, H, TN), BF16),
                dma((D // KT, KS)), dma((NA,)), dma((2,)),
                dma((2,)), dma((NX,)),
                dma((NS,)), dma((NE,)), dma((NM2,)),
                dma((NS, 4)), dma((NF,)), dma((NS, 2)), dma((NF,)), dma((NO,)),
            ],
            compiler_params=pltpu.CompilerParams(
                collective_id=1, has_side_effects=True, vmem_limit_bytes=43_900_000),
            name="sums",
        )(a, g)
        return pl.pallas_call(
            put,
            out_shape=jax.ShapeDtypeStruct((NM, D, F), BF16),
            in_specs=[pl.BlockSpec(memory_space=pltpu.VMEM)],
            out_specs=pl.BlockSpec(memory_space=pltpu.HBM),
            scratch_shapes=[dma((NM,))],
            compiler_params=pltpu.CompilerParams(vmem_limit_bytes=2**20),
            name="put",
        )(x)

    def step(a, g):
        return jax.shard_map(
            lambda a, g: sums(a[0], g[0]), mesh=mesh,
            in_specs=(P(("rep", "dp")), P(("rep", "dp"))), out_specs=P("rep"), check_vma=False)(a, g)

    return step
```

time: 302 us -> 293 us (0.970)
  local copies, waits for them, and re-layouts: 19.8 us -> 0 us
  Pallas kernels: 282 us -> 293 us
    unnamed x1 -> x0, local copies, waits for them, and re-layouts: 19.8 us -> none
    pallas_call x1 -> x2, Pallas kernels: 282 us -> 293 us  [the longest x1 285 us: sums(): pl.pallas_call(kernel, out_shape=(pltpu.VMEM((NM, D, F), BF16), jax.Shape...]
where the time goes in v2:
time: 293 us
  Pallas kernels  293 us (100%)
    pallas_call x1, Pallas kernels, sums(): pl.pallas_call(kernel, out_shape=(pltpu.VMEM((NM, D, F), BF16), jax.Shape...  285 us
    pallas_call x1, Pallas kernels, sums(): pl.pallas_call(put, out_shape=jax.ShapeDtypeStruct((NM, D, F), BF16), in_...  7.93 us

profile of v2, /device:TPU:0, one launch (start us, length us, event | category | flops | bytes accessed | tf_op | source)
XLA Modules:
  0.0 293.0 jit_solution(2233321722081398418)
XLA Ops:
  0.0 284.9 %sums.1 = (bf16[4,1024,2816]{2,1,0:T(8,128)(2,1)S(1)}, bf16[3,1024,2816]{2,1,0:T(8,128)(2,1)}) custom-call(bf16[4,8192,1024]{2,1,0:T(8,128)(2,1)} %bitcast.a, bf16[4,8192,2816]{2,1,0:T(8,128)(2,1)} %bitcast.1.g), custom_call_target="tpu_custom_call" | custom-call | tf_op jit(solution)/shard_map/sums/pallas_call | solution.py:378
  284.9 7.9 %put.1 = bf16[4,1024,2816]{2,1,0:T(8,128)(2,1)} custom-call(bf16[4,1024,2816]{2,1,0:T(8,128)(2,1)S(1)} %get-tuple-element.6.x), custom_call_target="tpu_custom_call" | custom-call | tf_op jit(solution)/shard_map/put/pallas_call | solution.py:403

commit v3 on v2

--- a/solution.py
+++ b/solution.py
@@ -14,6 +14,7 @@
 KT = 256
 KS = T // KT
 HB = TM // KT
+HG = 4
 KB = 512
 NB = T // KB
 KD = 8
@@ -51,7 +52,7 @@
         return x.at[k // J, rows, pl.ds(pl.multiple_of(k % J * TN, TN), TN)]
 
     def odd(k, rows):
-        return at1.at[k, rows, :]
+        return at1.at[pl.ds(pl.multiple_of(k * D + rows.start, KT), rows.size), :]
 
     ats = (even, odd)
 
@@ -63,9 +64,9 @@
         cols = pl.ds(pl.multiple_of(lax.rem(u, J) * TN, TN), TN)
         return pltpu.make_async_copy(g.at[u // J, :, cols], gbuf.at[lax.rem(u, 2)], gsem.at[lax.rem(u, 2)])
 
-    def hcopy(i, k):
-        rows = pl.ds(i * KT, KT)
-        return pltpu.make_async_copy(a.at[0, pl.ds(k * KT, KT), rows], at1.at[k, rows, :], hsem.at[i, k])
+    def hcopy(i, first, tokens, which):
+        return pltpu.make_async_copy(
+            a.at[0, pl.ds(first, tokens), pl.ds(i * KT, KT)], at1.at[pl.ds(i * T + first, tokens), :], hsem.at[which])
 
     def dot(at, rows, gb):
         total = None
@@ -250,37 +251,25 @@
     def _():
         pl.semaphore_signal(barrier, inc=1, device_id=dev(z + 1, c), device_id_type=MESH)
 
-    def fetch(r):
-        def one(k, _):
-            for i in range(r * HB, (r + 1) * HB):
-                hcopy(i, k).start()
-            return 0
-
-        lax.fori_loop(0, KS, one, 0)
-
-    def await_first(r, k):
-        for i in range(r * HB, (r + 1) * HB):
-            hcopy(i, k).wait()
-
-    def turn_first(r, k):
-        for i in range(r * HB, (r + 1) * HB):
-            rows = pl.ds(i * KT, KT)
-            even(k, rows)[...] = at1[k, rows, :].T
-
-    fetch(0)
+    def turn_first(i, k):
+        rows = pl.ds(i * KT, KT)
+        even(k, rows)[...] = at1[pl.ds(pl.multiple_of(i * T + k * KT, KT), KT), :].T
+
+    HT = T // HG
+    firsts = [hcopy(0, i * HT, HT, i) for i in range(HG)]
+    for copy in firsts:
+        copy.start()
     gcopy(0).start()
-    for r in range(1, R):
-        fetch(r)
+    parts = [None] + [hcopy(i, 0, T, HG - 1 + i) for i in range(1, D // KT)]
+    for copy in parts[1:]:
+        copy.start()
     for b in range(NA - 1 if RUN > 1 else 0):
         acopy(1, b).start()
     gcopy(1).start()
-
-    def first(k, _):
-        await_first(0, k)
-        turn_first(0, k)
-        return 0
-
-    lax.fori_loop(0, KS, first, 0)
+    for i, copy in enumerate(firsts):
+        copy.wait()
+        for k in range(i * KS // HG, (i + 1) * KS // HG):
+            turn_first(0, k)
 
     @pl.when(end)
     def _():
@@ -291,15 +280,17 @@
         pl.semaphore_wait(barrier, 3)
 
     gcopy(0).wait()
-    for r in range(R):
-        serve(jnp.int32(r))
-        if r < R - 1:
+    for i in range(D // KT):
+        r, rows = i // HB, pl.ds(i % HB * KT, KT)
+        if i % HB == 0:
+            serve(jnp.int32(r))
+        if i < D // KT - 1:
+            parts[i + 1].wait()
             for k in range(KS):
-                await_first(r + 1, k)
-            for k in range(KS):
-                turn_first(r + 1, k)
-        pb[r % NP] = dot(even, pl.ds(r * TM, TM), gbuf.at[0])
-        stage_x(jnp.int32(r))
+                turn_first(i + 1, k)
+        pb[r % NP, rows, :] = dot(even, pl.ds(i * KT, KT), gbuf.at[0])
+        if i % HB == HB - 1:
+            stage_x(jnp.int32(r))
 
     for n in range(RUN):
         now, later = ats[n % 2], ats[(n + 1) % 2]
@@ -381,7 +372,7 @@
             in_specs=[pl.BlockSpec(memory_space=pltpu.HBM)] * 2,
             out_specs=(pl.BlockSpec(memory_space=pltpu.VMEM), pl.BlockSpec(memory_space=pltpu.HBM)),
             scratch_shapes=[
-                pltpu.VMEM((KS, D, KT), BF16),
+                pltpu.VMEM((KS * D, KT), BF16),
                 pltpu.VMEM((2, T, TN), BF16),
                 pltpu.VMEM((NA, KB, D), BF16),
                 pltpu.VMEM((NP, TM, TN), F32),
@@ -391,7 +382,7 @@
                 pltpu.VMEM((NE, H, TN), BF16),
                 pltpu.VMEM((NM2, H, TN), BF16),
                 pltpu.VMEM((NS, H, TN), BF16),
-                dma((D // KT, KS)), dma((NA,)), dma((2,)),
+                dma((HG + D // KT - 1,)), dma((NA,)), dma((2,)),
                 dma((2,)), dma((NX,)),
                 dma((NS,)), dma((NE,)), dma((NM2,)),
                 dma((NS, 4)), dma((NF,)), dma((NS, 2)), dma((NF,)), dma((NO,)),

time: 293 us -> 288 us (0.983)
  Pallas kernels: 293 us -> 287 us
    pallas_call x1, Pallas kernels: 285 us -> 279 us  [sums(): pl.pallas_call(kernel, out_shape=(pltpu.VMEM((NM, D, F), BF16), jax.Shape...]
where the time goes in v3:
time: 288 us; the launch traced here: 287 us
  Pallas kernels  287 us (100%)
    pallas_call x1, Pallas kernels, sums(): pl.pallas_call(kernel, out_shape=(pltpu.VMEM((NM, D, F), BF16), jax.Shape...  279 us
    pallas_call x1, Pallas kernels, sums(): pl.pallas_call(put, out_shape=jax.ShapeDtypeStruct((NM, D, F), BF16), in_...  7.93 us

profile of v3, /device:TPU:0, one launch (start us, length us, event | category | flops | bytes accessed | tf_op | source)
XLA Modules:
  0.0 287.4 jit_solution(5813285059366321130)
XLA Ops:
  0.0 279.3 %sums.1 = (bf16[4,1024,2816]{2,1,0:T(8,128)(2,1)S(1)}, bf16[3,1024,2816]{2,1,0:T(8,128)(2,1)}) custom-call(bf16[4,8192,1024]{2,1,0:T(8,128)(2,1)} %bitcast.a, bf16[4,8192,2816]{2,1,0:T(8,128)(2,1)} %bitcast.1.g), custom_call_target="tpu_custom_call" | custom-call | tf_op jit(solution)/shard_map/sums/pallas_call | solution.py:369
  279.3 7.9 %put.1 = bf16[4,1024,2816]{2,1,0:T(8,128)(2,1)} custom-call(bf16[4,1024,2816]{2,1,0:T(8,128)(2,1)S(1)} %get-tuple-element.6.x), custom_call_target="tpu_custom_call" | custom-call | tf_op jit(solution)/shard_map/put/pallas_call | solution.py:394

commit v4 on v3

--- a/solution.py
+++ b/solution.py
@@ -25,11 +25,19 @@
 RUN = NM
 S = RUN * SM
 SX = (NM - 1) * SM
-NX, NE, NM2 = 11, 10, 4
+NX, NE, NM2 = 11, 10, 8
 NF = 16
 NP = 7
 NS = 4
-LX, LE, LM, LF, LG, LH = 2, 4, 6, 8, 10, 12
+NU = 2
+HU = H // NU
+LX, LE, LM, LF, LG, LH = 2, 3, 5, 7, 9, 11
+
+
+def when(condition):
+    if isinstance(condition, bool):
+        return lambda do: do() if condition else None
+    return pl.when(condition)
 
 
 def kernel(a, g, x, o, at1, gbuf, araw, pb, xs, xr, es, er, mr, fs, hsem, asem, gsem,
@@ -46,6 +54,8 @@
     z_end = jnp.where(z == 1, 0, 3)
     z_other = jnp.where(z == 1, 2, 1)
     inward = dev(jnp.where(end, z_mid, z_other), c)
+    near = jnp.where(end, z_mid, z) - 1
+    far = 1 - near
     sibling = dev(z, 1 - c)
 
     def even(k, rows):
@@ -85,52 +95,56 @@
         i, k = lax.rem(u, NX), lax.rem(u, 2)
         return remote(xs.at[k], xr.at[i], xss.at[k], xrs.at[i], sibling)
 
-    def ecopy(u):
+    def part(p):
+        return pl.ds(pl.multiple_of(p * HU, HU), HU)
+
+    def ecopy(u, p):
         i, k = lax.rem(u, NE), lax.rem(u, NS)
-        return remote(es.at[k], er.at[i], ess.at[k], ers.at[i], inward)
+        return remote(es.at[k, part(p)], er.at[i, part(p)], ess.at[k, p], ers.at[i, p], inward)
 
     def mcopy(u):
-        i, k = lax.rem(u // 2, NM2), lax.rem(u, NS)
-        return remote(es.at[k], mr.at[i], ess.at[k], mrs.at[i], inward)
-
-    def fcopies(u, at):
+        i, k = lax.rem(u, NM2), lax.rem(u, NS)
+        return remote(es.at[k, part(far)], mr.at[i], ess.at[k, far], mrs.at[i], inward)
+
+    def fcopies(u, p, at):
         i, k = lax.rem(u, NF), lax.rem(u, NS)
+        src = fs.at[k]
         return (
-            remote(fs.at[k], at, fss.at[k, 0], frs.at[i], dev(z_end, c)),
-            remote(fs.at[k], at, fss.at[k, 1], frs.at[i], dev(z_other, c)),
-            remote(fs.at[k], at, fss.at[k, 2], hrs.at[i], sibling),
+            remote(src, at, fss.at[k, 0], frs.at[i, p], dev(z_end, c)),
+            remote(src, at, fss.at[k, 1], frs.at[i, p], dev(z_other, c)),
+            remote(src, at, fss.at[k, 2], hrs.at[i, p], sibling),
         )
 
     def fkeep(u, at):
         k = lax.rem(u, NS)
         return pltpu.make_async_copy(fs.at[k], at, fss.at[k, 3])
 
-    def onward(u, at):
+    def onward(u, p, at):
         i, k = lax.rem(u, NF), lax.rem(u, NS)
-        return remote(at, at, gss.at[k, 0], frs.at[i], dev(z_end, c))
-
-    def across(u, at):
+        return remote(at, at, gss.at[k, p, 0], frs.at[i, p], dev(z_end, c))
+
+    def across(u, p, at):
         i, k = lax.rem(u, NF), lax.rem(u, NS)
-        return remote(at, at, gss.at[k, 1], hrs.at[i], sibling)
-
-    def placed(u, do):
+        return remote(at, at, gss.at[k, p, 1], hrs.at[i, p], sibling)
+
+    some = er.at[0, pl.ds(0, HU)]
+
+    def placed(u, p, early, do):
         q = lax.rem(u, SM)
-        rows = pl.ds(pl.multiple_of(lax.rem(q, R) * TM + c * H, H), H)
+        rows = pl.ds(pl.multiple_of(lax.rem(q, R) * TM + c * H + p * HU, HU), HU)
         cols = pl.ds(pl.multiple_of(q // R * TN, TN), TN)
 
-        @pl.when(u < SX)
+        @when(u < SX if early is None else early)
         def _():
             do(o.at[u // SM, rows, cols])
 
-        @pl.when(u >= SX)
+        @when(u >= SX if early is None else not early)
         def _():
             do(x.at[NM - 1, rows, cols])
 
-    def mine(u):
-        return z == 1 + lax.rem(u, 2)
-
-    def chip_sum(u):
-        return pb[lax.rem(u, NP), pl.ds(pl.multiple_of(c * H, H), H), :] + xr[lax.rem(u, NX)].astype(F32)
+    def chip_sum(u, p):
+        own = pb[lax.rem(u, NP), pl.ds(pl.multiple_of(c * H + p * HU, HU), HU), :]
+        return own + xr[lax.rem(u, NX), part(p), :].astype(F32)
 
     def live(u):
         return (u >= 0) & (u < S)
@@ -145,95 +159,100 @@
             xs[lax.rem(u, 2)] = pb[lax.rem(u, NP), pl.ds(pl.multiple_of((1 - c) * H, H), H), :].astype(BF16)
             xcopy(u).start()
 
-    def stage_end(u):
-        @pl.when(end & live(u - NS))
-        def _():
-            ecopy(u - NS).wait_send()
-
-        @pl.when(end & live(u))
+    def stage_end(u, sure):
+        @when(sure or live(u - NS))
+        def _():
+            for p in (far, near):
+                ecopy(u - NS, p).wait_send()
+
+        @when(sure or live(u))
         def _():
             xcopy(u).wait_recv()
-            es[lax.rem(u, NS)] = chip_sum(u).astype(BF16)
-            ecopy(u).start()
-
-    def stage_pass(u):
-        pass_on = mid & ~mine(u)
-
-        @pl.when(pass_on & live(u - NS))
+            for p in (far, near):
+                es[lax.rem(u, NS), part(p), :] = chip_sum(u, p).astype(BF16)
+                ecopy(u, p).start()
+
+    def stage_pass(u, sure):
+        @when(sure or live(u - NS))
         def _():
             mcopy(u - NS).wait_send()
 
-        @pl.when(pass_on & live(u))
+        @when(sure or live(u))
         def _():
             xcopy(u).wait_recv()
-            ecopy(u).wait_recv()
-            es[lax.rem(u, NS)] = (chip_sum(u) + er[lax.rem(u, NE)].astype(F32)).astype(BF16)
+            ecopy(u, far).wait_recv()
+            es[lax.rem(u, NS), part(far), :] = (
+                chip_sum(u, far) + er[lax.rem(u, NE), part(far), :].astype(F32)).astype(BF16)
             mcopy(u).start()
 
-    def stage_own(u):
-        k = lax.rem(u, NS)
-
-        @pl.when(mid & mine(u) & live(u - NS))
-        def _():
-            for copy in fcopies(u - NS, er.at[0]):
+    def stage_own(u, sure, early):
+        @when(sure or live(u - NS))
+        def _():
+            for copy in fcopies(u - NS, near, some):
                 copy.wait_send()
-            fkeep(u - NS, er.at[0]).wait()
-
-        @pl.when(mid & mine(u) & live(u))
-        def _():
-            xcopy(u).wait_recv()
-            ecopy(u).wait_recv()
+            fkeep(u - NS, some).wait()
+
+        @when(sure or live(u))
+        def _():
+            ecopy(u, near).wait_recv()
             mcopy(u).wait_recv()
-            fs[k] = (chip_sum(u) + er[lax.rem(u, NE)].astype(F32) + mr[lax.rem(u // 2, NM2)].astype(F32)).astype(BF16)
+            chips = chip_sum(u, near) + er[lax.rem(u, NE), part(near), :].astype(F32)
+            fs[lax.rem(u, NS)] = (chips + mr[lax.rem(u, NM2)].astype(F32)).astype(BF16)
 
             def send(at):
-                for copy in fcopies(u, at):
+                for copy in fcopies(u, near, at):
                     copy.start()
                 fkeep(u, at).start()
 
-            placed(u, send)
-
-    def stage_forward(u):
-        pass_on = mid & ~mine(u)
-
-        @pl.when(pass_on & live(u - NS))
-        def _():
-            onward(u - NS, er.at[0]).wait_send()
-            across(u - NS, er.at[0]).wait_send()
-
-        @pl.when(pass_on & live(u))
-        def _():
-            onward(u, er.at[0]).wait_recv()
+            placed(u, near, early, send)
+
+    def stage_forward(u, sure, early):
+        @when(sure or live(u - NS))
+        def _():
+            onward(u - NS, far, some).wait_send()
+            across(u - NS, far, some).wait_send()
+
+        @when(sure or live(u))
+        def _():
+            onward(u, far, some).wait_recv()
 
             def send(at):
-                onward(u, at).start()
-                across(u, at).start()
-
-            placed(u, send)
-
-    def stage_last(u):
-
-        @pl.when(end & live(u - NS))
-        def _():
-            across(u - NS, er.at[0]).wait_send()
-
-        @pl.when(end & live(u))
-        def _():
-            onward(u, er.at[0]).wait_recv()
-            placed(u, lambda at: across(u, at).start())
-
-    def stage_home(u):
-        @pl.when(live(u))
-        def _():
-            across(u, er.at[0]).wait_recv()
-
-    def serve(s):
-        stage_end(s - LX)
-        stage_own(s - LM)
-        stage_forward(s - LF)
-        stage_pass(s - LE)
-        stage_last(s - LG)
-        stage_home(s - LH)
+                onward(u, far, at).start()
+                across(u, far, at).start()
+
+            placed(u, far, early, send)
+
+    def stage_last(u, sure, early):
+        @when(sure or live(u - NS))
+        def _():
+            for p in (near, far):
+                across(u - NS, p, some).wait_send()
+
+        @when(sure or live(u))
+        def _():
+            for p in (near, far):
+                onward(u, p, some).wait_recv()
+                placed(u, p, early, lambda at, p=p: across(u, p, at).start())
+
+    def stage_home(u, sure):
+        @when(sure or live(u))
+        def _():
+            for p in range(NU):
+                across(u, p, some).wait_recv()
+
+    def serve(s, sure=False, early=None):
+        @pl.when(end)
+        def _():
+            stage_end(s - LX, sure)
+            stage_last(s - LG, sure, early)
+
+        @pl.when(mid)
+        def _():
+            stage_own(s - LM, sure, early)
+            stage_forward(s - LF, sure, early)
+            stage_pass(s - LE, sure)
+
+        stage_home(s - LH, sure)
 
     def take(p):
         cols = pl.ds(pl.multiple_of(lax.rem(p, J) * TN, TN), TN)
@@ -283,7 +302,7 @@
     for i in range(D // KT):
         r, rows = i // HB, pl.ds(i % HB * KT, KT)
         if i % HB == 0:
-            serve(jnp.int32(r))
+            serve(jnp.int32(r), early=True)
         if i < D // KT - 1:
             parts[i + 1].wait()
             for k in range(KS):
@@ -334,7 +353,7 @@
                     def _(p=p):
                         take(p).start()
 
-            serve(s)
+            serve(s, n > 0, True if n < NM - 1 else None)
             if n < RUN - 1:
                 for i in range(KB // KT):
                     for part in range(D // 256):
@@ -348,7 +367,7 @@
 
     def drain(s, _):
         stage_x(s)
-        serve(s)
+        serve(s, early=SX >= S)
         return 0
 
     lax.fori_loop(S, S + LH + NS, drain, 0)
@@ -380,12 +399,12 @@
                 pltpu.VMEM((NX, H, TN), BF16),
                 pltpu.VMEM((NS, H, TN), BF16),
                 pltpu.VMEM((NE, H, TN), BF16),
-                pltpu.VMEM((NM2, H, TN), BF16),
-                pltpu.VMEM((NS, H, TN), BF16),
+                pltpu.VMEM((NM2, HU, TN), BF16),
+                pltpu.VMEM((NS, HU, TN), BF16),
                 dma((HG + D // KT - 1,)), dma((NA,)), dma((2,)),
                 dma((2,)), dma((NX,)),
-                dma((NS,)), dma((NE,)), dma((NM2,)),
-                dma((NS, 4)), dma((NF,)), dma((NS, 2)), dma((NF,)), dma((NO,)),
+                dma((NS, NU)), dma((NE, NU)), dma((NM2,)),
+                dma((NS, 4)), dma((NF, NU)), dma((NS, NU, 2)), dma((NF, NU)), dma((NO,)),
             ],
             compiler_params=pltpu.CompilerParams(
                 collective_id=1, has_side_effects=True, vmem_limit_bytes=43_900_000),

time: 288 us -> 286 us (level)
  no operation moved by 1% of the time
where the time goes in v4:
time: 286 us
  Pallas kernels  285 us (100%)
    pallas_call x1, Pallas kernels, sums(): pl.pallas_call(kernel, out_shape=(pltpu.VMEM((NM, D, F), BF16), jax.Shape...  277 us
    pallas_call x1, Pallas kernels, sums(): pl.pallas_call(put, out_shape=jax.ShapeDtypeStruct((NM, D, F), BF16), in_...  7.93 us

profile of v4, /device:TPU:0, one launch (start us, length us, event | category | flops | bytes accessed | tf_op | source)
XLA Modules:
  0.0 285.5 jit_solution(3219501451821890205)
XLA Ops:
  0.0 277.4 %sums.1 = (bf16[4,1024,2816]{2,1,0:T(8,128)(2,1)S(1)}, bf16[3,1024,2816]{2,1,0:T(8,128)(2,1)}) custom-call(bf16[4,8192,1024]{2,1,0:T(8,128)(2,1)} %bitcast.a, bf16[4,8192,2816]{2,1,0:T(8,128)(2,1)} %bitcast.1.g), custom_call_target="tpu_custom_call" | custom-call | tf_op jit(solution)/shard_map/sums/pallas_call | solution.py:388
  277.5 7.9 %put.1 = bf16[4,1024,2816]{2,1,0:T(8,128)(2,1)} custom-call(bf16[4,1024,2816]{2,1,0:T(8,128)(2,1)S(1)} %get-tuple-element.6.x), custom_call_target="tpu_custom_call" | custom-call | tf_op jit(solution)/shard_map/put/pallas_call | solution.py:413

commit v5 on v4

--- a/solution.py
+++ b/solution.py
@@ -159,18 +159,21 @@
             xs[lax.rem(u, 2)] = pb[lax.rem(u, NP), pl.ds(pl.multiple_of((1 - c) * H, H), H), :].astype(BF16)
             xcopy(u).start()
 
+    def end_sum(u):
+        xcopy(u).wait_recv()
+        for p in (far, near):
+            es[lax.rem(u, NS), part(p), :] = chip_sum(u, p).astype(BF16)
+            ecopy(u, p).start()
+
     def stage_end(u, sure):
         @when(sure or live(u - NS))
         def _():
             for p in (far, near):
                 ecopy(u - NS, p).wait_send()
 
-        @when(sure or live(u))
-        def _():
-            xcopy(u).wait_recv()
-            for p in (far, near):
-                es[lax.rem(u, NS), part(p), :] = chip_sum(u, p).astype(BF16)
-                ecopy(u, p).start()
+        @when(sure or live(u) & (u > 0))
+        def _():
+            end_sum(u)
 
     def stage_pass(u, sure):
         @when(sure or live(u - NS))
@@ -307,6 +310,11 @@
             parts[i + 1].wait()
             for k in range(KS):
                 turn_first(i + 1, k)
+        else:
+            @pl.when(end)
+            def _():
+                end_sum(jnp.int32(0))
+
         pb[r % NP, rows, :] = dot(even, pl.ds(i * KT, KT), gbuf.at[0])
         if i % HB == HB - 1:
             stage_x(jnp.int32(r))

time: 286 us -> 288 us (level)
  no operation moved by 1% of the time
where the time goes in v5:
time: 288 us
  Pallas kernels  287 us (100%)
    pallas_call x1, Pallas kernels, sums(): pl.pallas_call(kernel, out_shape=(pltpu.VMEM((NM, D, F), BF16), jax.Shape...  280 us
    pallas_call x1, Pallas kernels, sums(): pl.pallas_call(put, out_shape=jax.ShapeDtypeStruct((NM, D, F), BF16), in_...  7.93 us

profile of v5, /device:TPU:0, one launch (start us, length us, event | category | flops | bytes accessed | tf_op | source)
XLA Modules:
  0.0 287.7 jit_solution(14719403604143111631)
XLA Ops:
  0.0 279.6 %sums.1 = (bf16[4,1024,2816]{2,1,0:T(8,128)(2,1)S(1)}, bf16[3,1024,2816]{2,1,0:T(8,128)(2,1)}) custom-call(bf16[4,8192,1024]{2,1,0:T(8,128)(2,1)} %bitcast.a, bf16[4,8192,2816]{2,1,0:T(8,128)(2,1)} %bitcast.1.g), custom_call_target="tpu_custom_call" | custom-call | tf_op jit(solution)/shard_map/sums/pallas_call | solution.py:396
  279.6 7.9 %put.1 = bf16[4,1024,2816]{2,1,0:T(8,128)(2,1)} custom-call(bf16[4,1024,2816]{2,1,0:T(8,128)(2,1)S(1)} %get-tuple-element.6.x), custom_call_target="tpu_custom_call" | custom-call | tf_op jit(solution)/shard_map/put/pallas_call | solution.py:421
